TPU v7x, 32 devices: a whole 2x2x4 slice. The times are simulated.
32 devices in a mesh: rep: 1, dp: 32 (over x, y, z, core).
Axes of the slice: x: 2, y: 2, z: 4, core: 2. Of those that a mesh axis runs over, the one named last changes fastest.
Arguments:
- x: bfloat16 [32, 2048, 1024], P(('rep', 'dp'))
- dy: bfloat16 [32, 2048, 1024], P(('rep', 'dp'))
- w_gate: bfloat16 [2, 1024, 3328], replicated
- w_up: bfloat16 [2, 1024, 3328], replicated
- w_down: bfloat16 [2, 3328, 1024], replicated
- m_w_gate: float32 [2, 1024, 3328], P(None, 'dp')
- m_w_up: float32 [2, 1024, 3328], P(None, 'dp')
- m_w_down: float32 [2, 3328, 1024], P(None, 'dp')
- v_w_gate: float32 [2, 1024, 3328], P(None, 'dp')
- v_w_up: float32 [2, 1024, 3328], P(None, 'dp')
- v_w_down: float32 [2, 3328, 1024], P(None, 'dp')
Outputs:
- output 1: bfloat16 [2, 1024, 3328], P('rep')
- output 2: bfloat16 [2, 1024, 3328], P('rep')
- output 3: bfloat16 [2, 3328, 1024], P('rep')
- output 4: float32 [2, 1024, 3328], P('rep', 'dp')
- output 5: float32 [2, 1024, 3328], P('rep', 'dp')
- output 6: float32 [2, 3328, 1024], P('rep', 'dp')
- output 7: float32 [2, 1024, 3328], P('rep', 'dp')
- output 8: float32 [2, 1024, 3328], P('rep', 'dp')
- output 9: float32 [2, 3328, 1024], P('rep', 'dp')
All inputs are finite; a program needn't handle non-finite values.
Results may differ from a plain program's by a relative error of at most 0.022.
Values are sent between devices in bfloat16 or wider.
A program may use at most 2 GiB of HBM per device.

v0:
```python
import jax
import jax.numpy as jnp
from jax import lax
from jax.experimental import pallas as pl
from jax.experimental.pallas import tpu as pltpu
from jax.sharding import PartitionSpec as P

BF, F32 = jnp.bfloat16, jnp.float32
MESH = pl.DeviceIdType.MESH

ROUTE = ("A", "A", "B", "B", "Cx", "Cy")
END = (65, 36, 8, 81, 52, 24, 1, 84, 72, 17, 4, 40, 33, 20, 56, 49, 68, 88, 69, 73, 12, 44, 66, 37, 9, 85, 89, 28, 60, 82, 53, 92, 25, 5, 76, 41, 2, 21, 57, 18, 74, 45, 77, 70, 34, 13, 50, 93, 86, 90, 29, 61, 67, 38, 10, 6, 42, 58, 22, 78, 83, 54, 26, 94, 75, 71, 14, 46, 3, 19, 91, 62, 87, 30, 35, 79, 51, 95, 43, 7, 39, 11, 23, 59, 15, 47, 55, 27, 31, 63)
MID = (65, 66, 36, 8, 81, 82, 52, 24, 1, 2, 84, 72, 17, 18, 4, 40, 33, 34, 20, 56, 49, 50, 68, 88, 37, 9, 67, 69, 73, 38, 70, 74, 10, 12, 44, 53, 25, 83, 85, 89, 54, 86, 90, 26, 28, 60, 3, 92, 5, 19, 6, 76, 41, 42, 35, 51, 21, 57, 22, 58, 39, 11, 45, 13, 75, 46, 55, 27, 71, 77, 14, 78, 61, 29, 91, 93, 62, 94, 87, 30, 7, 43, 23, 59, 15, 47, 63, 31, 79, 95)

def at(x, y, z, c):
    return ((x * 2 + y) * 4 + z) * 2 + c

class Place:
    def __init__(self):
        me = lax.axis_index("dp")
        self.me = me
        self.x, self.y, self.z, self.c = x, y, z, c = me // 16, me // 8 % 2, me // 2 % 4, me % 2
        self.end = (z == 0) | (z == 3)
        low = z < 2
        self.planes = (z, jnp.where(z == 0, 1, jnp.where(z == 1, 0, jnp.where(z == 2, 3, 2))), jnp.where(low, 2, 1), jnp.where(low, 3, 0))
        inner = jnp.where(z == 0, 1, jnp.where(z == 1, 2, jnp.where(z == 2, 1, 2)))
        outer = jnp.where(low, 0, 3)
        self.own = {"x": x, "y": y, "zh": z // 2, "zl": z % 2, "c": c}
        self.to = {"zl": at(x, y, z + 1 - 2 * (z % 2), c), "zh": at(x, y, (z + 2) % 4, c), "x": at(1 - x, y, z, c), "y": at(x, 1 - y, z, c), "core": at(x, y, z, 1 - c), "in": at(x, y, inner, c), "out": at(x, y, outer, c)}

    def chip(self, dx, dy, s):
        x = 1 - self.x if dx else self.x
        y = 1 - self.y if dy else self.y
        return (x * 2 + y) * 4 + self.planes[s]

def onward(route, dx, dy, s, end):
    z = {0: ["in"] if end else ["out", "in"], 1: [] if end else ["in"], 2: [] if end else ["out"], 3: [] if end else ["out"]}[s]
    own = (dx, dy, s) == (0, 0, 0)
    first, second = ("x", "y") if route in ("A", "Cx") else ("y", "x")
    near = dy == 0 if first == "x" else dx == 0
    side = dx if first == "x" else dy
    if route in "AB":
        if own: return [first, *z, second]
        if not near: return []
        return [*z, second]
    if not near: return []
    if side: return [second]
    return [*z, first, second]

def signal(sem, device):
    pl.semaphore_signal(sem, inc=1, device_id={"dp": device}, device_id_type=MESH)

def START(end):
    zz = ["in"] if end else ["out", "in"]
    A, B, X, Y = (0, 1), (2, 3), (4,), (5,)
    o = [(p, l) for p in X + Y for l in zz]
    o += [(p, "x") for p in A] + [(p, "y") for p in B] + [(p, l) for p in A + B for l in zz]
    o += [(p, "x") for p in X] + [(p, "y") for p in Y] + [(p, "x") for p in B + Y] + [(p, "y") for p in A + X]
    return o + [(p, "core") for p in range(6)]

def gather_refs(here, outs, sends, link, core):
    def region(p, owner):
        ref = outs[p // 2]
        rows = ref.shape[1] // 32
        return ref.at[p % 2, pl.ds(pl.multiple_of(owner * rows, 8), rows), :]
    def run(end):
        started = []
        def send(p, chip, to):
            r = region(p, chip * 2 + here.c)
            cp = pltpu.make_async_remote_copy(r, r, sends.at[len(started)], (core if to == "core" else link).at[p, chip], device_id={"dp": here.to[to]}, device_id_type=MESH)
            started.append(cp)
            cp.start()
        def wait(p, owner, sem):
            pltpu.make_async_copy(region(p, owner), region(p, owner), sem).wait()
        mine = here.chip(0, 0, 0)
        for p, to in START(end): send(p, mine, to)
        for code in END if end else MID:
            p, dx, dy, s = code // 16, code // 8 % 2, code // 4 % 2, code % 4
            chip = here.chip(dx, dy, s)
            wait(p, chip * 2 + here.c, link.at[p, chip])
            for to in onward(ROUTE[p], dx, dy, s, end) + ["core"]: send(p, chip, to)
        def landed(chip, _):
            for p in range(6): wait(p, chip * 2 + 1 - here.c, core.at[p, chip])
            return 0
        lax.fori_loop(0, 16, landed, 0)
        for cp in started: cp.wait_send()
    @pl.when(here.end)
    def _(): run(True)
    @pl.when(jnp.logical_not(here.end))
    def _(): run(False)


XY, YX, ZX, ZY = ("x", "y", "zl", "zh"), ("y", "x", "zl", "zh"), ("zl", "x", "y", "zh"), ("zl", "y", "x", "zh")
WEIGHT = {"x": 8, "y": 4, "zh": 2, "zl": 1}
EVENTS = (1, 9, 17, 25, 33, 41, 2, 49, 10, 57, 18, 65, 26, 42, 34, 3, 66, 50, 4, 11, 5, 58, 19, 12, 27, 13, 35, 43, 28, 67, 36, 29, 51, 37, 59, 20, 44, 68, 52, 60, 21, 45, 69, 53, 61)


def streams(mats):
    out = []
    for m, ref in enumerate(mats):
        tiles = ref.shape[-1] // 128
        a, b = 128 * -(-tiles // 3), 128 * (-(-tiles // 3) + -(-(tiles - -(-tiles // 3)) // 2))
        out += [(m, 0, a, XY), (m, a, b - a, YX), (m, b, 128 * tiles - b, ZY if m % 2 else ZX)]
    return out


def sum_scratch(mats):
    out = []
    for m, _, w, _ in streams(mats):
        rows = mats[m].shape[-2]
        out += [pltpu.VMEM((16, rows, w), BF), pltpu.VMEM((31, rows, w), BF), pltpu.VMEM((15, rows, w), BF)]
    n = len(streams(mats))
    return [*out, pltpu.SemaphoreType.DMA((n,)), pltpu.SemaphoreType.DMA((n, 5)), pltpu.SemaphoreType.DMA((n, 5))]


class Sum:
    def __init__(self, here, mats, outs, scratch):
        self.here, self.mats, self.outs = here, mats, outs
        self.streams = streams(mats)
        n = len(self.streams)
        self.held = [scratch[3 * s : 3 * s + 3] for s in range(n)]
        self.local, self.sent, self.got = scratch[3 * n :]
        self.copies = {}

    def part(self, s, core):
        m, first, w, _ = self.streams[s]
        return self.mats[m].at[:, core, :, first : first + w]

    def send(self, s, j):
        here = self.here
        own, came, goes = self.held[s]
        order = ("core", *self.streams[s][3])
        n = 16 >> j
        src = self.part(s, 1 - here.c) if j == 0 else goes.at[16 - 2 * n : 16 - n]
        cp = pltpu.make_async_remote_copy(src, came.at[32 - 2 * n : 32 - n], self.sent.at[s, j], self.got.at[s, j], device_id={"dp": here.to[order[j]]}, device_id_type=MESH)
        self.copies[s, j] = cp
        cp.start()

    def start(self):
        for s in range(len(self.streams)):
            self.send(s, 0)
            pltpu.make_async_copy(self.part(s, self.here.c), self.held[s][0], self.local.at[s]).start()

    def event(self, code):
        s, j = code // 8, code % 8
        m, first, w, order = self.streams[s]
        own, came, goes = self.held[s]
        mine = self.here.own
        if j == 1:
            pltpu.make_async_copy(self.part(s, self.here.c), own, self.local.at[s]).wait()
        self.copies[s, j - 1].wait_recv()
        away = 0 if j == 5 else 1 - mine[order[j - 1]]

        def block(k):
            b = sum(mine[o] * WEIGHT[o] for o in order[: j - 1])
            if j < 5:
                b = b + away * WEIGHT[order[j - 1]]
            b = b + sum(k // 2 ** (3 - i) % 2 * WEIGHT[order[i]] for i in range(j, 4))
            total = own[b].astype(F32) + came[b].astype(F32)
            for i in range(1, j):
                at_i = 32 - (32 >> i) + sum(mine[order[t]] * 2 ** (3 - t) for t in range(i, j - 1)) + k
                if j < 5:
                    at_i = at_i + away * 2 ** (4 - j)
                total = total + came[at_i].astype(F32)
            return total.astype(BF)

        if j == 5:
            self.outs[m][:, first : first + w] = block(0)
            return
        n = 16 >> j

        def one(k, _):
            goes[16 - 2 * n + k] = block(k)
            return 0

        lax.fori_loop(0, n, one, 0)
        self.send(s, j)

    def finish(self):
        for cp in self.copies.values():
            cp.wait_send()


def entry(here):
    sem = pltpu.get_barrier_semaphore()
    for link in ("x", "y", "core", "zl", "zh"):
        signal(sem, here.to[link])
    mid = jnp.logical_not(here.end)

    @pl.when(mid)
    def _():
        signal(sem, here.to["in"])

    pl.semaphore_wait(sem, jnp.where(mid, 6, 5))


def blocks(g):
    return g.reshape(16, 2, g.shape[0] // 32, g.shape[1])


ANY, VMEM = pl.BlockSpec(memory_space=pl.ANY), pl.BlockSpec(memory_space=pltpu.VMEM)


def scattered(*g):
    g = [blocks(t) for t in g]

    def kernel(*refs):
        here = Place()
        total = Sum(here, refs[:3], refs[3:6], refs[6:])
        entry(here)
        total.start()
        for code in EVENTS:
            total.event(code)
        total.finish()

    return pl.pallas_call(
        kernel,
        out_shape=[jax.ShapeDtypeStruct(t.shape[2:], BF) for t in g],
        in_specs=[ANY] * 3,
        out_specs=[VMEM] * 3,
        scratch_shapes=sum_scratch(g),
        name="scattered",
        compiler_params=pltpu.CompilerParams(collective_id=1, has_side_effects=True, vmem_limit_bytes=56 << 20),
    )(*g)


def tiles(ref, width=256):
    def each(f):
        def one(i, carry):
            return f(pl.ds(pl.multiple_of(i * width, width), width), carry)

        return lambda carry: lax.fori_loop(0, ref.shape[-1] // width, one, carry)

    return each


def stepped(g1, g0, w, m, v):
    g0 = [blocks(t) for t in g0]
    count = sum(t.size for t in w)

    def kernel(*refs):
        g1, g0, w, m, v = (refs[i : i + 3] for i in range(0, 15, 3))
        new, new_m, new_v = (refs[i : i + 3] for i in range(15, 24, 3))
        r0, own_w, stage = (refs[i : i + 3] for i in range(24, 33, 3))
        norms, load, sends, link, core, nsent, ngot = refs[33:40]
        here = Place()
        total = Sum(here, g0, r0, refs[40:])
        entry(here)
        total.start()

        def rows_of(ref, p):
            rows = r0[p // 2].shape[0]
            return ref.at[p % 2, pl.ds(pl.multiple_of(here.me * rows, 8), rows), :]

        for p in range(6):
            pltpu.make_async_copy(rows_of(w[p // 2], p), own_w[p // 2].at[p % 2], load.at[p]).start()
        for code in EVENTS:
            total.event(code)

        squares = jnp.zeros((8, 128), F32)
        for ref in (*g1, *r0):
            def add(cols, so_far, ref=ref):
                g = ref[:, cols].astype(F32)
                g = (g * g).reshape(-1, 8, 2, 128)
                return so_far + jnp.sum(g[:, :, 0] + g[:, :, 1], 0)
            squares = tiles(ref)(add)(squares)
        squares = jnp.broadcast_to(jnp.sum(jnp.sum(squares, 0, keepdims=True), 1, keepdims=True), (8, 128))
        for k, to in enumerate(("core", "x", "y", "zl", "zh")):
            norms[k] = squares
            cp = pltpu.make_async_remote_copy(norms.at[k], norms.at[5 + k], nsent.at[k], ngot.at[k], device_id={"dp": here.to[to]}, device_id_type=MESH)
            cp.start()
            cp.wait()
            squares = squares + norms[5 + k]
        factor = jnp.minimum(1.0, 0.5 * lax.rsqrt(squares / count + 1e-30))[:1, :1]

        for p in range(6):
            a, n = p // 2, p % 2
            pltpu.make_async_copy(rows_of(w[a], p), own_w[a].at[n], load.at[p]).wait()
            g_ref = (g1 if n else r0)[a]

            def one(cols, _, a=a, n=n, g_ref=g_ref):
                g = g_ref[:, cols].astype(F32) * factor
                wide = own_w[a][n, :, cols].astype(F32)
                stage[a][n, :, cols], new_m[a][n, :, cols], new_v[a][n, :, cols] = adamw(wide, m[a][n, :, cols], v[a][n, :, cols], g)
                return 0

            tiles(g_ref)(one)(0)
            pltpu.make_async_copy(stage[a].at[n], rows_of(new[a], p), load.at[p]).start()
        for p in range(6):
            pltpu.make_async_copy(stage[p // 2].at[p % 2], rows_of(new[p // 2], p), load.at[p]).wait()
        gather_refs(here, new, sends, link, core)
        total.finish()

    state = [jax.ShapeDtypeStruct(t.shape, F32) for t in m]
    return pl.pallas_call(
        kernel,
        out_shape=[*(jax.ShapeDtypeStruct(t.shape, BF) for t in w), *state, *state],
        in_specs=[*[VMEM] * 3, *[ANY] * 6, *[VMEM] * 6],
        out_specs=[*[ANY] * 3, *[VMEM] * 6],
        scratch_shapes=[
            *(pltpu.VMEM(t.shape[2:], BF) for t in g0),
            *(pltpu.VMEM(t.shape, BF) for t in m),
            *(pltpu.VMEM(t.shape, BF) for t in m),
            pltpu.VMEM((10, 8, 128), F32),
            pltpu.SemaphoreType.DMA((6,)),
            pltpu.SemaphoreType.DMA((240,)),
            pltpu.SemaphoreType.DMA((6, 16)),
            pltpu.SemaphoreType.DMA((6, 16)),
            pltpu.SemaphoreType.DMA((5,)),
            pltpu.SemaphoreType.DMA((5,)),
            *sum_scratch(g0),
        ],
        name="stepped",
        compiler_params=pltpu.CompilerParams(collective_id=2, has_side_effects=True, vmem_limit_bytes=63 << 20),
    )(*g1, *g0, *w, *m, *v)


def dot(a, b, contract):
    return lax.dot_general(a, b, ((contract[:1], contract[1:]), ((), ())), preferred_element_type=F32)


def normed(h):
    wide = h.astype(F32)
    scale = lax.rsqrt(jnp.mean(wide**2, -1, keepdims=True) + 1e-6)
    return (wide * scale).astype(BF), scale


def gates(gate, up, by_hidden):
    by = by_hidden.astype(F32)
    sigmoid = jax.nn.sigmoid(gate)
    by_gate = by * up * (sigmoid * (1 + gate * (1 - sigmoid)))
    return by_gate.astype(BF), (by * gate * sigmoid).astype(BF)


def adamw(w, m, v, g):
    m = 0.9 * m + 0.1 * g
    v = 0.95 * v + 0.05 * g * g
    step = m * lax.rsqrt(v + 1e-8) + 0.1 * w
    return (w - 0.02 * step).astype(BF), m, v


def solution(mesh):
    def step(x, dy, *arrays):
        w, m, v = (arrays[i : i + 3] for i in (0, 3, 6))
        h, by = x[0], dy[0]
        layers, kept = w[0].shape[0], []
        for n in range(layers):
            a, scale = normed(h)
            gate, up = dot(a, w[0][n], (1, 0)), dot(a, w[1][n], (1, 0))
            hidden = (jax.nn.silu(gate) * up).astype(BF)
            kept.append((h, a, scale, gate, up, hidden))
            if n + 1 < layers:
                h = h + dot(hidden, w[2][n], (1, 0)).astype(BF)
        sums = [None] * layers
        for n in reversed(range(layers)):
            h, a, scale, gate, up, hidden = kept[n]
            by_down = dot(hidden, by, (0, 0)).astype(BF)
            by_hidden = dot(by, w[2][n], (1, 1)).astype(BF)
            by_gate, by_up = gates(gate, up, by_hidden)
            sums[n] = dot(a, by_gate, (0, 0)).astype(BF), dot(a, by_up, (0, 0)).astype(BF), by_down
            if n:
                by_a = dot(by_gate, w[0][n], (1, 1)).astype(BF) + dot(by_up, w[1][n], (1, 1)).astype(BF)
                wide, by_a = h.astype(F32), by_a.astype(F32)
                inner = jnp.mean(by_a * wide, -1, keepdims=True)
                by = by + (by_a * scale - wide * (scale**3 * inner)).astype(BF)
        return tuple(stepped(scattered(*sums[1]), sums[0], w, m, v))

    rows = P(None, "dp", None)
    return jax.shard_map(
        step,
        mesh=mesh,
        in_specs=(P(("rep", "dp")), P(("rep", "dp")), *(P(),) * 3, *(rows,) * 6),
        out_specs=(*(P("rep"),) * 3, *(P("rep", "dp", None),) * 6),
        check_vma=False,
    )
```

profile of v0, /device:TPU:1, one launch (start us, length us, event | category | flops | bytes accessed | tf_op | source)
XLA Modules:
  0.0 785.0 jit_solution(9132866703110858523)
XLA Ops:
  0.6 6.5 copy.20
  7.2 3.1 fusion.13
  10.3 0.0 copy-start.13
  10.3 6.5 copy.21
  16.8 20.9 %convolution_convert_fusion.1 = bf16[2048,3328]{1,0:T(8,128)(2,1)} fusion(bf16[2,3328,1024]{2,1,0:T(8,128)(2,1)} %refs_8_.1, bf16[1,2048,1024]{2,1,0:T(8,128)(2,1)} %param.12), kind=kOutput, calls=%fused_computation.17 | convolution fusion | flops 13965459456 | bytes 24641536 | tf_op jit(solution)/shard_map/dot_general | solution.py:319
  37.7 0.0 copy-start.4
  37.7 22.2 %fusion.41 = f32[2048,3328]{1,0:T(8,128)} fusion(bf16[2,1024,3328]{2,1,0:T(8,128)(2,1)} %refs_6_.1, bf16[1,2048,1024]{2,1,0:T(8,128)(2,1)} %param.11, f32[2048]{0:T(1024)S(1)} %add_rsqrt_fusion.1), kind=kOutput, calls=%fused_computation.56 | convolution fusion | flops 13964935168 | bytes 38281216 | tf_op jit(solution)/shard_map/dot_general | solution.py:319
  60.0 0.0 copy-done.13
  60.0 0.0 copy-done.4
  60.0 28.8 %multiply_convert_fusion.1 = (bf16[2048,3328]{1,0:T(8,128)(2,1)}, f32[2048,3328]{1,0:T(8,128)}) fusion(f32[2048,3328]{1,0:T(8,128)} %fusion.41, bf16[2,1024,3328]{2,1,0:T(8,128)(2,1)} %refs_7_.1, bf16[1,2048,1024]{2,1,0:T(8,128)(2,1)S(1)} %copy-done.4, f32[2048]{0:T(1024)S(1)} %add_rsqrt_fusion.1), kind=kOutput, calls=%fused_computation.14 | convolution fusion | flops 14005829632 | bytes 79175680 | tf_op jit(solution)/shard_map/dot_general | solution.py:319
  88.8 22.1 %fusion.17 = (f32[2048]{0:T(1024)S(1)}, bf16[2048,1024]{0,1:T(8,128)(2,1)}) fusion(bf16[2048,3328]{1,0:T(8,128)(2,1)} %get-tuple-element.17, bf16[2,3328,1024]{2,1,0:T(8,128)(2,1)} %refs_8_.1, bf16[1,2048,1024]{1,2,0:T(8,128)(2,1)} %copy.20), kind=kOutput, calls=%fused_computation.32 | convolution fusion | flops 13969127424 | bytes 28844032 | tf_op jit(solution)/shard_map/dot_general | solution.py:319
  110.9 0.0 copy-start.11
  110.9 23.6 %fusion.33 = f32[2048,3328]{1,0:T(8,128)} fusion(bf16[2,1024,3328]{2,1,0:T(8,128)(2,1)} %refs_7_.1, bf16[2048,1024]{0,1:T(8,128)(2,1)} %get-tuple-element.20, f32[2048]{0:T(1024)S(1)} %add_rsqrt_fusion), kind=kOutput, calls=%fused_computation.48 | convolution fusion | flops 13964935168 | bytes 38281216 | tf_op jit(solution)/shard_map/dot_general | solution.py:319
  134.5 0.0 copy-done.11
  134.5 43.3 %fusion.3 = (bf16[2048,3328]{1,0:T(8,128)(2,1)}, bf16[2048,3328]{1,0:T(8,128)(2,1)}, f32[2048,3328]{1,0:T(8,128)}) fusion(bf16[2048,3328]{1,0:T(8,128)(2,1)} %convolution_convert_fusion.1, f32[2048,3328]{1,0:T(8,128)} %fusion.33, bf16[2,1024,3328]{2,1,0:T(8,128)(2,1)} %refs_6_.1, bf16[2048,1024]{0,1:T(8,128)(2,1)} %get-tuple-element.20, ...), kind=kOutput, calls=%fused_computation.7 | convolution fusion | flops 14060355584 | bytes 106438656 | tf_op jit(solution)/shard_map/dot_general | solution.py:319
  177.8 27.0 %fusion.26 = bf16[3328,1024]{1,0:T(8,128)(2,1)} fusion(f32[2048,3328]{1,0:T(8,128)} %fusion.33, f32[2048,3328]{1,0:T(8,128)} %get-tuple-element.21, bf16[1,2048,1024]{2,1,0:T(8,128)(2,1)} %param.12), kind=kOutput, calls=%fused_computation.38 | convolution fusion | flops 14002946048 | bytes 65536000 | tf_op jit(solution)/shard_map/dot_general | solution.py:319
  204.8 0.0 copy-start.2
  204.8 0.0 copy-start.15
  204.8 20.3 %fusion.27 = bf16[2048,1024]{0,1:T(8,128)(2,1)} fusion(bf16[2048,3328]{1,0:T(8,128)(2,1)} %get-tuple-element.16, bf16[2,1024,3328]{2,1,0:T(8,128)(2,1)} %refs_6_.1), kind=kOutput, calls=%fused_computation.42 | convolution fusion | flops 13958643712 | bytes 24641536 | tf_op jit(solution)/shard_map/dot_general | solution.py:319
  225.1 0.0 copy-done.2
  225.1 0.0 copy-done.15
  225.1 16.2 %convolution_convert_fusion.4 = bf16[1024,3328]{1,0:T(8,128)(2,1)} fusion(bf16[2048,3328]{1,0:T(8,128)(2,1)S(1)} %copy-done.15, bf16[2048,1024]{0,1:T(8,128)(2,1)S(1)} %copy-done.2, f32[2048]{0:T(1024)S(1)} %add_rsqrt_fusion), kind=kOutput, calls=%fused_computation.41 | convolution fusion | flops 13968343040 | bytes 24649728 | tf_op jit(solution)/shard_map/dot_general | solution.py:319
  241.3 22.9 %fusion.19 = (f32[2048]{0:T(1024)S(1)}, bf16[2048,1024]{0,1:T(8,128)(2,1)}) fusion(bf16[2048,1024]{0,1:T(8,128)(2,1)} %get-tuple-element.20, bf16[2048,1024]{0,1:T(8,128)(2,1)} %fusion.27, bf16[2048,3328]{1,0:T(8,128)(2,1)} %get-tuple-element.15, bf16[2,1024,3328]{2,1,0:T(8,128)(2,1)} %refs_7_.1), kind=kOutput, calls=%fused_computation.34 | convolution fusion | flops 13971224576 | bytes 33038336 | tf_op jit(solution)/shard_map/dot_general | solution.py:319
  264.2 21.2 %convolution_convert_fusion.3 = bf16[1024,3328]{1,0:T(8,128)(2,1)} fusion(bf16[2048,3328]{1,0:T(8,128)(2,1)} %get-tuple-element.15, bf16[2048,1024]{0,1:T(8,128)(2,1)} %get-tuple-element.20, f32[2048]{0:T(1024)S(1)} %add_rsqrt_fusion), kind=kOutput, calls=%fused_computation.40 | convolution fusion | flops 13968343040 | bytes 24649728 | tf_op jit(solution)/shard_map/dot_general | solution.py:319
  285.4 0.0 copy-start.12
  285.4 0.0 copy-start
  285.4 98.2 %scattered.1 = (bf16[32,3328]{1,0:T(8,128)(2,1)}, bf16[32,3328]{1,0:T(8,128)(2,1)}, bf16[104,1024]{1,0:T(8,128)(2,1)}) custom-call(bf16[16,2,32,3328]{3,2,1,0:T(8,128)(2,1)} %bitcast.76, bf16[16,2,32,3328]{3,2,1,0:T(8,128)(2,1)} %bitcast.77, bf16[16,2,104,1024]{3,2,1,0:T(8,128)(2,1)} %bitcast.75), custom_call_target="tpu_custom_call" | custom-call | tf_op jit(solution)/shard_map/scattered/pallas_call | solution.py:216
  383.6 0.0 copy-done.12
  383.7 0.0 copy-done
  383.7 5.4 fusion.53
  389.0 0.0 copy-start.3
  389.1 20.9 %convolution_convert_fusion.2 = bf16[3328,1024]{1,0:T(8,128)(2,1)} fusion(bf16[2048,3328]{1,0:T(8,128)(2,1)} %get-tuple-element.17, bf16[2048,1024]{0,1:T(8,128)(2,1)S(1)} %fusion.53), kind=kOutput, calls=%fused_computation.39 | convolution fusion | flops 13962051584 | bytes 24641536 | tf_op jit(solution)/shard_map/dot_general | solution.py:319
  409.9 0.0 copy-done.3
  409.9 0.0 copy-start.14
  409.9 21.2 %convolution_convert_fusion = bf16[2048,3328]{1,0:T(8,128)(2,1)} fusion(bf16[2048,1024]{0,1:T(8,128)(2,1)} %copy-done.3, bf16[2,3328,1024]{2,1,0:T(8,128)(2,1)} %refs_8_.1), kind=kOutput, calls=%fused_computation.16 | convolution fusion | flops 13965459456 | bytes 24641536 | tf_op jit(solution)/shard_map/dot_general | solution.py:319
  431.1 0.0 copy-done.14
  431.2 30.7 %fusion.20 = bf16[1024,3328]{1,0:T(8,128)(2,1)} fusion(f32[2048,3328]{1,0:T(8,128)} %get-tuple-element.18, bf16[2048,3328]{1,0:T(8,128)(2,1)} %convolution_convert_fusion, f32[2048,3328]{1,0:T(8,128)} %fusion.41, bf16[1,2048,1024]{1,2,0:T(8,128)(2,1)} %copy.20, f32[2048]{0:T(1024)S(1)} %copy-done.14), kind=kOutput, calls=%fused_computation.36 | convolution fusion | flops 14043316224 | bytes 79175680 | tf_op jit(solution)/shard_map/dot_general | solution.py:319
  461.9 25.1 %fusion.23 = bf16[1024,3328]{1,0:T(8,128)(2,1)} fusion(f32[2048,3328]{1,0:T(8,128)} %fusion.41, bf16[2048,3328]{1,0:T(8,128)(2,1)} %convolution_convert_fusion, bf16[1,2048,1024]{1,2,0:T(8,128)(2,1)} %copy.20, f32[2048]{0:T(1024)S(1)} %copy-done.14), kind=kOutput, calls=%fused_computation.37 | convolution fusion | flops 14016053248 | bytes 51912704 | tf_op jit(solution)/shard_map/dot_general | solution.py:319
  487.0 263.7 %stepped.1 = (bf16[2,1024,3328]{2,1,0:T(8,128)(2,1)}, bf16[2,1024,3328]{2,1,0:T(8,128)(2,1)}, bf16[2,3328,1024]{2,1,0:T(8,128)(2,1)}, f32[2,32,3328]{2,1,0:T(8,1...) custom-call(bf16[32,3328]{1,0:T(8,128)(2,1)} %get-tuple-element.12.r, ...), custom_call_target="tpu_custom_call" | custom-call | tf_op jit(solution)/shard_map/stepped/pallas_call | solution.py:295
  750.8 0.0 copy-start.1
  750.8 0.0 slice-start
  750.8 0.0 slice-start.1
  750.8 15.1 %copy.31 = bf16[2,1024,3328]{2,1,0:T(8,128)(2,1)} copy(bf16[2,1024,3328]{2,1,0:T(8,128)(2,1)} %get-tuple-element.33) | data formatting | bytes 27262976
  765.8 0.0 copy-done.1
  765.9 6.5 copy.32
  772.4 0.0 slice-done
  772.4 0.0 slice-done.1
  772.4 0.0 slice-done.2
  772.4 0.4 slice-done.3
  772.8 0.0 copy-start.6
  772.9 0.0 copy-start.5
  772.9 6.3 copy.33
  779.2 0.0 copy-done.10
  779.2 0.9 copy.34
  780.1 0.0 copy-done.9
  780.1 0.9 copy.35
  781.0 0.0 copy-done.8
  781.0 0.9 copy.36
  781.9 0.0 copy-done.7
  781.9 0.9 copy.37
  782.8 0.0 copy-done.6
  782.8 0.9 copy.38
  783.7 0.0 copy-done.5
  783.7 0.9 copy.39
  (10 shorter events, 0.0 us)
Async XLA Ops:
  10.3 49.7 %copy-start.13 = (f32[2048]{0:T(1024)}, f32[2048]{0:T(1024)S(1)}, u32[]{:S(2)}) copy-start(f32[2048]{0:T(1024)S(1)} %add_rsqrt_fusion.1) | copy-start | bytes 24580
  37.7 22.2 %copy-start.4 = (bf16[1,2048,1024]{2,1,0:T(8,128)(2,1)S(1)}, bf16[1,2048,1024]{2,1,0:T(8,128)(2,1)}, u32[]{:S(2)}) copy-start(bf16[1,2048,1024]{2,1,0:T(8,128)(2,1)} %param.11) | copy-start | bytes 12582916
  110.9 23.6 %copy-start.11 = (f32[2048]{0:T(1024)}, f32[2048]{0:T(1024)S(1)}, u32[]{:S(2)}) copy-start(f32[2048]{0:T(1024)S(1)} %get-tuple-element.19) | copy-start | bytes 24580
  204.8 20.3 %copy-start.2 = (bf16[2048,1024]{0,1:T(8,128)(2,1)S(1)}, bf16[2048,1024]{0,1:T(8,128)(2,1)}, u32[]{:S(2)}) copy-start(bf16[2048,1024]{0,1:T(8,128)(2,1)} %get-tuple-element.20) | copy-start | bytes 12582916
  204.8 20.3 %copy-start.15 = (bf16[2048,3328]{1,0:T(8,128)(2,1)S(1)}, bf16[2048,3328]{1,0:T(8,128)(2,1)}, u32[]{:S(2)}) copy-start(bf16[2048,3328]{1,0:T(8,128)(2,1)} %get-tuple-element.16) | copy-start | bytes 40894468
  285.4 98.2 %copy-start.12 = (f32[2048]{0:T(1024)S(1)}, f32[2048]{0:T(1024)}, u32[]{:S(2)}) copy-start(f32[2048]{0:T(1024)} %copy-done.11) | copy-start | bytes 24580
  285.4 98.3 %copy-start = (bf16[1,2048,1024]{1,2,0:T(8,128)(2,1)S(1)}, bf16[1,2048,1024]{1,2,0:T(8,128)(2,1)}, u32[]{:S(2)}) copy-start(bf16[1,2048,1024]{1,2,0:T(8,128)(2,1)} %copy.21) | copy-start | bytes 12582916
  389.0 20.9 %copy-start.3 = (bf16[2048,1024]{0,1:T(8,128)(2,1)}, bf16[2048,1024]{0,1:T(8,128)(2,1)S(1)}, u32[]{:S(2)}) copy-start(bf16[2048,1024]{0,1:T(8,128)(2,1)S(1)} %fusion.53) | copy-start | bytes 12582916
  409.9 21.2 %copy-start.14 = (f32[2048]{0:T(1024)S(1)}, f32[2048]{0:T(1024)}, u32[]{:S(2)}) copy-start(f32[2048]{0:T(1024)} %copy-done.13) | copy-start | bytes 24580
  750.8 15.1 %copy-start.1 = (bf16[2,1024,3328]{2,1,0:T(8,128)(2,1)S(1)}, bf16[2,1024,3328]{2,1,0:T(8,128)(2,1)}, u32[]{:S(2)}) copy-start(bf16[2,1024,3328]{2,1,0:T(8,128)(2,1)} %get-tuple-element.34) | copy-start | bytes 40894468
  750.8 21.6 %slice-start = ((s8[13631488]{0:T(1024)(128)(4,1)}), s8[4194304]{0:T(1024)(128)(4,1)S(1)}, s32[]{:S(2)}) async-start(s8[13631488]{0:T(1024)(128)(4,1)} %bitcast.70), calls=%async_computation | async-start | bytes 8388608
  750.8 21.6 %slice-start.1 = ((s8[13631488]{0:T(1024)(128)(4,1)}), s8[4194304]{0:T(1024)(128)(4,1)S(1)}, s32[]{:S(2)}) async-start(s8[13631488]{0:T(1024)(128)(4,1)} %bitcast.70), calls=%async_computation.1 | async-start | bytes 8388608
  765.8 6.6 slice-start.2
  765.8 7.0 slice-start.3
  772.8 6.4 copy-start.10
  772.8 7.3 copy-start.9
  772.8 8.2 %copy-start.8 = (f32[2,104,1024]{2,1,0:T(8,128)S(1)}, f32[2,104,1024]{2,1,0:T(8,128)}, u32[]{:S(2)}) copy-start(f32[2,104,1024]{2,1,0:T(8,128)} %get-tuple-element.38) | copy-start | bytes 2555908
  772.8 9.1 %copy-start.7 = (f32[2,32,3328]{2,1,0:T(8,128)S(1)}, f32[2,32,3328]{2,1,0:T(8,128)}, u32[]{:S(2)}) copy-start(f32[2,32,3328]{2,1,0:T(8,128)} %get-tuple-element.39) | copy-start | bytes 2555908
  772.8 10.0 %copy-start.6 = (f32[2,32,3328]{2,1,0:T(8,128)S(1)}, f32[2,32,3328]{2,1,0:T(8,128)}, u32[]{:S(2)}) copy-start(f32[2,32,3328]{2,1,0:T(8,128)} %get-tuple-element.40) | copy-start | bytes 2555908
  772.9 10.8 %copy-start.5 = (f32[2,104,1024]{2,1,0:T(8,128)S(1)}, f32[2,104,1024]{2,1,0:T(8,128)}, u32[]{:S(2)}) copy-start(f32[2,104,1024]{2,1,0:T(8,128)} %get-tuple-element.41) | copy-start | bytes 2555908
where the time goes:
time: 793 us; the launch traced here: 785 us
  matrix products  366 us (46%)
  Pallas kernels  362 us (46%)
  local copies, waits for them, and re-layouts  46.9 us (6%)
  other arithmetic  8.44 us (1%)
    dot_general x15, matrix products, dot(): lax.dot_general(a, b, ((contract[:1], contract[1:]), ((), ())), preferred...  366 us
    pallas_call x1, Pallas kernels, stepped(): pl.pallas_call(kernel, out_shape=[*(jax.ShapeDtypeStruct(t.shape, BF) for...  264 us
    pallas_call x1, Pallas kernels, scattered(): pl.pallas_call(kernel, out_shape=[jax.ShapeDtypeStruct(t.shape[2:], BF) f...  98.2 us
    unnamed x51, local copies, waits for them, and re-layouts  46.9 us

commit v1 on v0

--- a/solution.py
+++ b/solution.py
@@ -93,6 +93,7 @@
 XY, YX, ZX, ZY = ("x", "y", "zl", "zh"), ("y", "x", "zl", "zh"), ("zl", "x", "y", "zh"), ("zl", "y", "x", "zh")
 WEIGHT = {"x": 8, "y": 4, "zh": 2, "zl": 1}
 EVENTS = (1, 9, 17, 25, 33, 41, 2, 49, 10, 57, 18, 65, 26, 42, 34, 3, 66, 50, 4, 11, 5, 58, 19, 12, 27, 13, 35, 43, 28, 67, 36, 29, 51, 37, 59, 20, 44, 68, 52, 60, 21, 45, 69, 53, 61)
+DUE = (2, 3, 4, 5, 6, 7, 8, 8, 9, 9, 9, 10, 12, 13, 13, 16, 17, 17, 18, 20, 20, 21, 22, 22, 23, 24, 24, 25, 25, 26, 26, 27, 28, 28, 28, 29, 29, 29, 30, 31, 32, 32, 33, 34, 34)
 
 
 def streams(mats):
@@ -108,7 +109,7 @@
     out = []
     for m, _, w, _ in streams(mats):
         rows = mats[m].shape[-2]
-        out += [pltpu.VMEM((16, rows, w), BF), pltpu.VMEM((31, rows, w), BF), pltpu.VMEM((15, rows, w), BF)]
+        out += [pltpu.VMEM((2, 8, rows, w), BF), pltpu.VMEM((2, 8, rows, w), BF), pltpu.VMEM((15, rows, w), BF)]
     n = len(streams(mats))
     return [*out, pltpu.SemaphoreType.DMA((n,)), pltpu.SemaphoreType.DMA((n, 5)), pltpu.SemaphoreType.DMA((n, 5))]
 
@@ -120,47 +121,74 @@
         n = len(self.streams)
         self.held = [scratch[3 * s : 3 * s + 3] for s in range(n)]
         self.local, self.sent, self.got = scratch[3 * n :]
-        self.copies = {}
-
-    def part(self, s, core):
-        m, first, w, _ = self.streams[s]
-        return self.mats[m].at[:, core, :, first : first + w]
-
-    def send(self, s, j):
+
+    def parts(self, s, core, to):
+        m, first, w, order = self.streams[s]
+        ref, cols = self.mats[m], slice(first, first + w)
+        if order[0] == "x":
+            return [(ref.at[8 * h : 8 * h + 8, core, :, cols], to.at[h]) for h in (0, 1)]
+        if order[0] == "y":
+            return [(ref.at[8 * x + 4 * h : 8 * x + 4 * h + 4, core, :, cols], to.at[h, 4 * x : 4 * x + 4]) for h in (0, 1) for x in (0, 1)]
+        return [(ref.at[b, core, :, cols], to.at[b % 2, b // 2]) for b in range(16)]
+
+    def from_core(self, s):
         here = self.here
-        own, came, goes = self.held[s]
-        order = ("core", *self.streams[s][3])
+        return [
+            pltpu.make_async_remote_copy(src, dst, self.sent.at[s, 0], self.got.at[s, 0], device_id={"dp": here.to["core"]}, device_id_type=MESH)
+            for src, dst in self.parts(s, 1 - here.c, self.held[s][1])
+        ]
+
+    def whole(self, s, semaphore):
+        ref = self.held[s][0]
+        pltpu.make_async_copy(ref, ref, semaphore).wait()
+
+    def copy(self, s, j):
+        here = self.here
+        own, core, came = self.held[s]
+        order = self.streams[s][3]
         n = 16 >> j
-        src = self.part(s, 1 - here.c) if j == 0 else goes.at[16 - 2 * n : 16 - n]
-        cp = pltpu.make_async_remote_copy(src, came.at[32 - 2 * n : 32 - n], self.sent.at[s, j], self.got.at[s, j], device_id={"dp": here.to[order[j]]}, device_id_type=MESH)
-        self.copies[s, j] = cp
-        cp.start()
+        away = 1 - here.own[order[0]]
+        src = own.at[away] if j == 1 else core.at[away, 8 - 2 * n : 8 - n]
+        return pltpu.make_async_remote_copy(src, came.at[16 - 2 * n : 16 - n], self.sent.at[s, j], self.got.at[s, j], device_id={"dp": here.to[order[j - 1]]}, device_id_type=MESH)
 
     def start(self):
         for s in range(len(self.streams)):
-            self.send(s, 0)
-            pltpu.make_async_copy(self.part(s, self.here.c), self.held[s][0], self.local.at[s]).start()
+            for cp in self.from_core(s):
+                cp.start()
+            for src, dst in self.parts(s, self.here.c, self.held[s][0]):
+                pltpu.make_async_copy(src, dst, self.local.at[s]).start()
 
     def event(self, code):
         s, j = code // 8, code % 8
         m, first, w, order = self.streams[s]
-        own, came, goes = self.held[s]
+        own, core, came = self.held[s]
         mine = self.here.own
+        rest = [o for o in ("x", "y", "zh", "zl") if o != order[0]]
+        weight = {o: 4 >> i for i, o in enumerate(rest)}
         if j == 1:
-            pltpu.make_async_copy(self.part(s, self.here.c), own, self.local.at[s]).wait()
-        self.copies[s, j - 1].wait_recv()
+            self.whole(s, self.local.at[s])
+            self.whole(s, self.got.at[s, 0])
+        else:
+            self.copy(s, j - 1).wait_recv()
         away = 0 if j == 5 else 1 - mine[order[j - 1]]
+        half = away if j == 1 else mine[order[0]]
+
+        def place(k):
+            b = sum(mine[o] * weight[o] for o in order[1 : j - 1])
+            if 1 < j < 5:
+                b = b + away * weight[order[j - 1]]
+            return b + sum(k // 2 ** (3 - i) % 2 * weight[order[i]] for i in range(j, 4))
 
         def block(k):
-            b = sum(mine[o] * WEIGHT[o] for o in order[: j - 1])
-            if j < 5:
-                b = b + away * WEIGHT[order[j - 1]]
-            b = b + sum(k // 2 ** (3 - i) % 2 * WEIGHT[order[i]] for i in range(j, 4))
-            total = own[b].astype(F32) + came[b].astype(F32)
+            b = place(k)
+            total = own[half, b].astype(F32) + core[half, b].astype(F32)
             for i in range(1, j):
-                at_i = 32 - (32 >> i) + sum(mine[order[t]] * 2 ** (3 - t) for t in range(i, j - 1)) + k
-                if j < 5:
-                    at_i = at_i + away * 2 ** (4 - j)
+                if i == 1:
+                    at_i = b
+                else:
+                    at_i = 16 - (32 >> i) + sum(mine[order[t]] * 2 ** (3 - t) for t in range(i, j - 1)) + k
+                    if j < 5:
+                        at_i = at_i + away * 2 ** (4 - j)
                 total = total + came[at_i].astype(F32)
             return total.astype(BF)
 
@@ -170,15 +198,20 @@
         n = 16 >> j
 
         def one(k, _):
-            goes[16 - 2 * n + k] = block(k)
+            if j == 1:
+                own[half, place(k)] = block(k)
+            else:
+                core[1 - mine[order[0]], 8 - 2 * n + k] = block(k)
             return 0
 
         lax.fori_loop(0, n, one, 0)
-        self.send(s, j)
+        self.copy(s, j).start()
 
     def finish(self):
-        for cp in self.copies.values():
-            cp.wait_send()
+        for s in range(len(self.streams)):
+            self.whole(s, self.sent.at[s, 0])
+            for j in range(1, 5):
+                self.copy(s, j).wait_send()
 
 
 def entry(here):
@@ -201,27 +234,195 @@
 ANY, VMEM = pl.BlockSpec(memory_space=pl.ANY), pl.BlockSpec(memory_space=pltpu.VMEM)
 
 
-def scattered(*g):
+TILE = 256
+PARAMS = {"vmem_limit_bytes": 63 << 20}
+
+
+def once(shape):
+    return pl.BlockSpec(shape, lambda t: (0,) * len(shape), pipeline_mode=pl.Buffered(1))
+
+
+def prepared(h, by):
+    tokens, d = h.shape
+    rows = 512
+
+    def kernel(h, by, a, a_t, by_t):
+        a[...] = normed(h[...])
+        a_t[...] = a[...].T
+        by_t[...] = by[...].T
+
+    short, tall = pl.BlockSpec((rows, d), lambda t: (t, 0)), pl.BlockSpec((d, rows), lambda t: (0, t))
+    flat, turned = jax.ShapeDtypeStruct((tokens, d), BF), jax.ShapeDtypeStruct((d, tokens), BF)
+    return pl.pallas_call(
+        kernel,
+        grid=(tokens // rows,),
+        out_shape=[flat, turned, turned],
+        in_specs=[short, short],
+        out_specs=[short, tall, tall],
+        name="prepared",
+        compiler_params=pltpu.CompilerParams(**PARAMS),
+    )(h, by)
+
+
+def forward_up(n, a, w_gate, w_up, hidden):
+    tokens, d = a.shape
+    ff = w_gate.shape[2]
+
+    def kernel(a, w_gate, w_up, gate, up, *hid):
+        rows = 512
+        for i in range(tokens // rows):
+            at_i = slice(i * rows, (i + 1) * rows)
+            g, u = dot(a[at_i, :], w_gate[...], (1, 0)), dot(a[at_i, :], w_up[...], (1, 0))
+            gate[at_i, :], up[at_i, :] = g, u
+            if hid:
+                hid[0][at_i, :] = (jax.nn.silu(g) * u).astype(BF)
+
+    tile, weight = pl.BlockSpec((tokens, TILE), lambda t: (0, t)), pl.BlockSpec((None, d, TILE), lambda t: (n, 0, t))
+    return pl.pallas_call(
+        kernel,
+        grid=(ff // TILE,),
+        out_shape=[jax.ShapeDtypeStruct((tokens, ff), t) for t in (F32, F32, BF)[: 2 + hidden]],
+        in_specs=[once((tokens, d)), weight, weight],
+        out_specs=[tile] * (2 + hidden),
+        name="forward_up",
+        compiler_params=pltpu.CompilerParams(**PARAMS),
+    )(a, w_gate, w_up)
+
+
+def forward_down(n, hidden, w_down, h):
+    tokens, ff = hidden.shape
+    d = h.shape[1]
+    rows = 512
+
+    def kernel(hidden, w_down, h, out, a, a_t):
+        out[...] = h[...] + dot(hidden[...], w_down[...], (1, 0)).astype(BF)
+        a[...] = normed(out[...])
+        a_t[...] = a[...].T
+
+    short, tall = pl.BlockSpec((rows, d), lambda t: (t, 0)), pl.BlockSpec((d, rows), lambda t: (0, t))
+    flat, turned = jax.ShapeDtypeStruct((tokens, d), BF), jax.ShapeDtypeStruct((d, tokens), BF)
+    return pl.pallas_call(
+        kernel,
+        grid=(tokens // rows,),
+        out_shape=[flat, flat, turned],
+        in_specs=[pl.BlockSpec((rows, ff), lambda t: (t, 0)), pl.BlockSpec((None, ff, d), lambda t: (n, 0, 0), pipeline_mode=pl.Buffered(1)), short],
+        out_specs=[short, short, tall],
+        name="forward_down",
+        compiler_params=pltpu.CompilerParams(**PARAMS),
+    )(hidden, w_down, h)
+
+
+def of_tile(by, by_t, a_t, gate, up, w_down, hid, by_gate, by_up, by_w, between=lambda: None):
+    rows = 512
+    for i in range(by.shape[0] // rows):
+        at_i = slice(i * rows, (i + 1) * rows)
+        by_hidden = dot(by[at_i, :], w_down[...], (1, 1)).astype(BF).astype(F32)
+        g, u = gate[at_i, :], up[at_i, :]
+        sigmoid = jax.nn.sigmoid(g)
+        silu = g * sigmoid
+        hid[at_i, :] = (silu * u).astype(BF)
+        by_up[at_i, :] = (by_hidden * silu).astype(BF)
+        by_gate[at_i, :] = (by_hidden * u * (sigmoid + silu * (1 - sigmoid))).astype(BF)
+    between()
+    by_w[0][...] = dot(a_t[...], by_gate[...], (1, 0)).astype(BF)
+    by_w[1][...] = dot(a_t[...], by_up[...], (1, 0)).astype(BF)
+    by_w[2][...] = dot(by_t[...], hid[...], (1, 0)).T.astype(BF)
+
+
+def backward(n, by, by_t, a_t, gate, up, w_down):
+    tokens, d = by.shape
+    ff = gate.shape[1]
+
+    def kernel(by, by_t, a_t, gate, up, w_down, *refs):
+        by_w, by_gate, by_up, hid = refs[:3], refs[3], refs[4], refs[5]
+        of_tile(by, by_t, a_t, gate, up, w_down, hid, by_gate, by_up, by_w)
+
+    tile = pl.BlockSpec((tokens, TILE), lambda t: (0, t))
+    return pl.pallas_call(
+        kernel,
+        grid=(ff // TILE,),
+        out_shape=[jax.ShapeDtypeStruct(s, BF) for s in ((d, ff), (d, ff), (ff, d), (tokens, ff), (tokens, ff))],
+        in_specs=[once((tokens, d)), once((d, tokens)), once((d, tokens)), tile, tile, pl.BlockSpec((None, TILE, d), lambda t: (n, t, 0))],
+        out_specs=[pl.BlockSpec((d, TILE), lambda t: (0, t))] * 2 + [pl.BlockSpec((TILE, d), lambda t: (t, 0)), tile, tile],
+        scratch_shapes=[pltpu.VMEM((tokens, TILE), BF)],
+        name="backward",
+        compiler_params=pltpu.CompilerParams(**PARAMS),
+    )(by, by_t, a_t, gate, up, w_down)
+
+
+def backward_beside(g, n, by, by_t, a_t, gate, up, w_down):
     g = [blocks(t) for t in g]
+    tokens, d = by.shape
+    ff = gate.shape[1]
+    steps = ff // TILE
 
     def kernel(*refs):
+        by, by_t, a_t, gate, up, w_down = refs[:6]
+        by_w, sums = refs[9:12], refs[12:15]
+        hid, by_gate, by_up = refs[15:18]
         here = Place()
-        total = Sum(here, refs[:3], refs[3:6], refs[6:])
-        entry(here)
-        total.start()
-        for code in EVENTS:
-            total.event(code)
-        total.finish()
-
-    return pl.pallas_call(
-        kernel,
-        out_shape=[jax.ShapeDtypeStruct(t.shape[2:], BF) for t in g],
-        in_specs=[ANY] * 3,
-        out_specs=[VMEM] * 3,
-        scratch_shapes=sum_scratch(g),
-        name="scattered",
-        compiler_params=pltpu.CompilerParams(collective_id=1, has_side_effects=True, vmem_limit_bytes=56 << 20),
-    )(*g)
+        total = Sum(here, refs[6:9], sums, refs[18:])
+        step = pl.program_id(0)
+
+        @pl.when(step == 0)
+        def _():
+            entry(here)
+            total.start()
+
+        def slot(part):
+            for t in range(steps):
+                due = [e for e, at_e in zip(EVENTS, DUE, strict=True) if min(at_e, 2 * steps - 1) == 2 * t + part]
+                if due:
+                    @pl.when(step == t)
+                    def _(due=due):
+                        for code in due:
+                            total.event(code)
+
+        of_tile(by, by_t, a_t, gate, up, w_down, hid, by_gate, by_up, by_w, lambda: slot(0))
+        slot(1)
+
+        @pl.when(step == steps - 1)
+        def _():
+            total.finish()
+
+    tile = pl.BlockSpec((tokens, TILE), lambda t: (0, t))
+    return pl.pallas_call(
+        kernel,
+        grid=(steps,),
+        out_shape=[*(jax.ShapeDtypeStruct(s, BF) for s in ((d, ff), (d, ff), (ff, d))), *(jax.ShapeDtypeStruct(t.shape[2:], BF) for t in g)],
+        in_specs=[once((tokens, d)), once((d, tokens)), once((d, tokens)), tile, tile, pl.BlockSpec((None, TILE, d), lambda t: (n, t, 0)), *[ANY] * 3],
+        out_specs=[pl.BlockSpec((d, TILE), lambda t: (0, t))] * 2 + [pl.BlockSpec((TILE, d), lambda t: (t, 0))] + [once(t.shape[2:]) for t in g],
+        scratch_shapes=[pltpu.VMEM((tokens, TILE), BF)] * 3 + sum_scratch(g),
+        name="backward_beside",
+        compiler_params=pltpu.CompilerParams(collective_id=1, has_side_effects=True, **PARAMS),
+    )(by, by_t, a_t, gate, up, w_down, *g)
+
+
+def backward_states(n, by_gate, by_up, w_gate, w_up, h, by):
+    tokens, d = by.shape
+    ff = by_gate.shape[1]
+    rows = 512
+
+    def kernel(by_gate, by_up, w_gate, w_up, h, by, out, out_t):
+        by_a = dot(by_gate[...], w_gate[...], (1, 1)).astype(BF) + dot(by_up[...], w_up[...], (1, 1)).astype(BF)
+        wide, by_a = h[...].astype(F32), by_a.astype(F32)
+        scale = lax.rsqrt(jnp.mean(wide**2, -1, keepdims=True) + 1e-6)
+        inner = jnp.mean(by_a * wide, -1, keepdims=True)
+        new = by[...] + (by_a * scale - wide * (scale**3 * inner)).astype(BF)
+        out[...] = new
+        out_t[...] = new.T
+
+    long, short = pl.BlockSpec((rows, ff), lambda t: (t, 0)), pl.BlockSpec((rows, d), lambda t: (t, 0))
+    weight = pl.BlockSpec((None, d, ff), lambda t: (n, 0, 0), pipeline_mode=pl.Buffered(1))
+    return pl.pallas_call(
+        kernel,
+        grid=(tokens // rows,),
+        out_shape=[jax.ShapeDtypeStruct((tokens, d), BF), jax.ShapeDtypeStruct((d, tokens), BF)],
+        in_specs=[long, long, weight, weight, short, short],
+        out_specs=[short, pl.BlockSpec((d, rows), lambda t: (0, t))],
+        name="backward_states",
+        compiler_params=pltpu.CompilerParams(**PARAMS),
+    )(by_gate, by_up, w_gate, w_up, h, by)
 
 
 def tiles(ref, width=256):
@@ -321,15 +522,7 @@
 
 def normed(h):
     wide = h.astype(F32)
-    scale = lax.rsqrt(jnp.mean(wide**2, -1, keepdims=True) + 1e-6)
-    return (wide * scale).astype(BF), scale
-
-
-def gates(gate, up, by_hidden):
-    by = by_hidden.astype(F32)
-    sigmoid = jax.nn.sigmoid(gate)
-    by_gate = by * up * (sigmoid * (1 + gate * (1 - sigmoid)))
-    return by_gate.astype(BF), (by * gate * sigmoid).astype(BF)
+    return (wide * lax.rsqrt(jnp.mean(wide**2, -1, keepdims=True) + 1e-6)).astype(BF)
 
 
 def adamw(w, m, v, g):
@@ -342,28 +535,15 @@
 def solution(mesh):
     def step(x, dy, *arrays):
         w, m, v = (arrays[i : i + 3] for i in (0, 3, 6))
-        h, by = x[0], dy[0]
-        layers, kept = w[0].shape[0], []
-        for n in range(layers):
-            a, scale = normed(h)
-            gate, up = dot(a, w[0][n], (1, 0)), dot(a, w[1][n], (1, 0))
-            hidden = (jax.nn.silu(gate) * up).astype(BF)
-            kept.append((h, a, scale, gate, up, hidden))
-            if n + 1 < layers:
-                h = h + dot(hidden, w[2][n], (1, 0)).astype(BF)
-        sums = [None] * layers
-        for n in reversed(range(layers)):
-            h, a, scale, gate, up, hidden = kept[n]
-            by_down = dot(hidden, by, (0, 0)).astype(BF)
-            by_hidden = dot(by, w[2][n], (1, 1)).astype(BF)
-            by_gate, by_up = gates(gate, up, by_hidden)
-            sums[n] = dot(a, by_gate, (0, 0)).astype(BF), dot(a, by_up, (0, 0)).astype(BF), by_down
-            if n:
-                by_a = dot(by_gate, w[0][n], (1, 1)).astype(BF) + dot(by_up, w[1][n], (1, 1)).astype(BF)
-                wide, by_a = h.astype(F32), by_a.astype(F32)
-                inner = jnp.mean(by_a * wide, -1, keepdims=True)
-                by = by + (by_a * scale - wide * (scale**3 * inner)).astype(BF)
-        return tuple(stepped(scattered(*sums[1]), sums[0], w, m, v))
+        h0, by = x[0], dy[0]
+        a0, a0_t, by_t = prepared(h0, by)
+        gate0, up0, hidden0 = forward_up(0, a0, w[0], w[1], True)
+        h1, a1, a1_t = forward_down(0, hidden0, w[2], h0)
+        gate1, up1 = forward_up(1, a1, w[0], w[1], False)
+        *g1, by_gate, by_up = backward(1, by, by_t, a1_t, gate1, up1, w[2])
+        by, by_t = backward_states(1, by_gate, by_up, w[0], w[1], h1, by)
+        both = backward_beside(g1, 0, by, by_t, a0_t, gate0, up0, w[2])
+        return tuple(stepped(both[3:], both[:3], w, m, v))
 
     rows = P(None, "dp", None)
     return jax.shard_map(

time: 793 us -> 636 us (0.80); the launches traced: 785 us -> 636 us
  matrix products: 366 us -> 0 us
  Pallas kernels: 362 us -> 602 us
  local copies, waits for them, and re-layouts: 46.9 us -> 33.8 us
  other arithmetic: 8.44 us -> 0.01 us
    dot_general x15 -> x0, matrix products: 366 us -> none  [dot(): lax.dot_general(a, b, ((contract[:1], contract[1:]), ((), ())), preferred...]
    pallas_call x1 -> x7, Pallas kernels: 98.2 us -> 337 us  [the longest x1 115 us: backward_beside(): pl.pallas_call(kernel, grid=(steps,), out_shape=[*(jax.ShapeDtypeStruct(s...]
    unnamed x51 -> x31, local copies, waits for them, and re-layouts: 46.9 us -> 33.8 us
where the time goes in v1:
time: 636 us
  Pallas kernels  602 us (95%)
  local copies, waits for them, and re-layouts  33.8 us (5%)
    pallas_call x1, Pallas kernels, stepped(): pl.pallas_call(kernel, out_shape=[*(jax.ShapeDtypeStruct(t.shape, BF) for...  264 us
    pallas_call x1, Pallas kernels, backward_beside(): pl.pallas_call(kernel, grid=(steps,), out_shape=[*(jax.ShapeDtypeStruct(s...  115 us
    pallas_call x1, Pallas kernels, backward(): pl.pallas_call(kernel, grid=(ff // TILE,), out_shape=[jax.ShapeDtypeStruc...  77.1 us
    pallas_call x2, Pallas kernels, forward_up(): pl.pallas_call(kernel, grid=(ff // TILE,), out_shape=[jax.ShapeDtypeStruc...  71.1 us
    pallas_call x1, Pallas kernels, backward_states(): pl.pallas_call(kernel, grid=(tokens // rows,), out_shape=[jax.ShapeDtypeS...  41.5 us
    unnamed x31, local copies, waits for them, and re-layouts  33.8 us
    pallas_call x1, Pallas kernels, forward_down(): pl.pallas_call(kernel, grid=(tokens // rows,), out_shape=[flat, flat, tur...  23.3 us

profile of v1, /device:TPU:1, one launch (start us, length us, event | category | flops | bytes accessed | tf_op | source)
XLA Modules:
  0.0 636.0 jit_solution(1255295043781236863)
XLA Ops:
  0.6 9.0 %prepared.1 = (bf16[2048,1024]{1,0:T(8,128)(2,1)}, bf16[1024,2048]{1,0:T(8,128)(2,1)}, bf16[1024,2048]{1,0:T(8,128)(2,1)}) custom-call(bf16[2048,1024]{1,0:T(8,128)(2,1)} %bitcast.11, bf16[2048,1024]{1,0:T(8,128)(2,1)} %bitcast.8), custom_call_target="tpu_custom_call" | custom-call | tf_op jit(solution)/shard_map/prepared/pallas_call | solution.py:256
  9.7 35.8 %forward_up.2 = (f32[2048,3328]{1,0:T(8,128)}, f32[2048,3328]{1,0:T(8,128)}, bf16[2048,3328]{1,0:T(8,128)(2,1)}) custom-call(bf16[2048,1024]{1,0:T(8,128)(2,1)} %get-tuple-element.34.a, bf16[2,1024,3328]{2,1,0:T(8,128)(2,1)} %refs_6_.1, bf16[2,1024,3328]{2,1,0:T(8,128)(2,1)} %refs_7_.1), custom_call_target="tpu_custom_call" | custom-call | tf_op jit(solution)/shard_map/forward_up/pallas_call | solution.py:281
  45.4 23.3 %forward_down.1 = (bf16[2048,1024]{1,0:T(8,128)(2,1)}, bf16[2048,1024]{1,0:T(8,128)(2,1)}, bf16[1024,2048]{1,0:T(8,128)(2,1)}) custom-call(bf16[2048,3328]{1,0:T(8,128)(2,1)} %get-tuple-element.35.hidden, bf16[2,3328,1024]{2,1,0:T(8,128)(2,1)} %refs_8_.1, bf16[2048,1024]{1,0:T(8,128)(2,1)} %bitcast.12), custom_call_target="tpu_custom_call" | custom-call | tf_op jit(solution)/shard_map/forward_down/pallas_call | solution.py:304
  68.7 35.4 %forward_up.3 = (f32[2048,3328]{1,0:T(8,128)}, f32[2048,3328]{1,0:T(8,128)}) custom-call(bf16[2048,1024]{1,0:T(8,128)(2,1)} %get-tuple-element.37.a, bf16[2,1024,3328]{2,1,0:T(8,128)(2,1)} %refs_6_.1, bf16[2,1024,3328]{2,1,0:T(8,128)(2,1)} %refs_7_.1), custom_call_target="tpu_custom_call" | custom-call | tf_op jit(solution)/shard_map/forward_up/pallas_call | solution.py:281
  104.1 77.1 %backward.1 = (bf16[1024,3328]{1,0:T(8,128)(2,1)}, bf16[1024,3328]{1,0:T(8,128)(2,1)}, bf16[3328,1024]{1,0:T(8,128)(2,1)}, bf16[2048,3328]{1,0:T(8,128)(2,1)}, bf16[2048,3328]{1,0:T(8,128)(2,1)}) custom-call(bf16[2048,1024]{1,0:T(8,128)(2,1)} %bitcast.9, bf16[1024,2048]{1,0:T(8,128)(2,1)} %get-tuple-element.33.by_t, ...), custom_call_target="tpu_custom_call" | custom-call | tf_op jit(solution)/shard_map/backward/pallas_call | solution.py:341
  181.2 41.5 %backward_states.1 = (bf16[2048,1024]{1,0:T(8,128)(2,1)}, bf16[1024,2048]{1,0:T(8,128)(2,1)}) custom-call(bf16[2048,3328]{1,0:T(8,128)(2,1)} %get-tuple-element.40.by_gate, bf16[2048,3328]{1,0:T(8,128)(2,1)} %get-tuple-element.41.by_up, bf16[2,1024,3328]{2,1,0:T(8,128)(2,1)} %refs_6_.1, bf16[2,1024,3328]{2,1,0:T(8,128)(2,1)} %refs_7_.1, ...), custom_call_target="tpu_custom_call" | custom-call | tf_op jit(solution)/shard_map/backward_states/pallas_call | solution.py:417
  222.7 115.1 %backward_beside.1 = (bf16[1024,3328]{1,0:T(8,128)(2,1)}, bf16[1024,3328]{1,0:T(8,128)(2,1)}, bf16[3328,1024]{1,0:T(8,128)(2,1)}, bf16[32,3328]{1,0:T(8,128)(2,1...) custom-call(bf16[2048,1024]{1,0:T(8,128)(2,1)} %get-tuple-element.43.refs_0_, ...), custom_call_target="tpu_custom_call" | custom-call | tf_op jit(solution)/shard_map/backward_beside/pallas_call | solution.py:389
  337.8 264.3 %stepped.1 = (bf16[2,1024,3328]{2,1,0:T(8,128)(2,1)}, bf16[2,1024,3328]{2,1,0:T(8,128)(2,1)}, bf16[2,3328,1024]{2,1,0:T(8,128)(2,1)}, f32[2,32,3328]{2,1,0:T(8,1...) custom-call(bf16[32,3328]{1,0:T(8,128)(2,1)} %get-tuple-element.51.r, ...), custom_call_target="tpu_custom_call" | custom-call | tf_op jit(solution)/shard_map/stepped/pallas_call | solution.py:496
  602.2 0.0 copy-start
  602.2 0.0 slice-start
  602.2 0.0 slice-start.1
  602.2 15.1 %copy.29 = bf16[2,1024,3328]{2,1,0:T(8,128)(2,1)} copy(bf16[2,1024,3328]{2,1,0:T(8,128)(2,1)} %get-tuple-element.66) | data formatting | bytes 27262976
  617.3 0.0 copy-done
  617.3 0.0 slice-start.2
  617.3 0.0 slice-start.3
  617.3 6.5 %copy.30 = bf16[2,1024,3328]{2,1,0:T(8,128)(2,1)} copy(bf16[2,1024,3328]{2,1,0:T(8,128)(2,1)S(1)} %copy-done) | data formatting | bytes 27262976
  623.8 0.0 slice-done
  623.8 0.0 slice-done.1
  623.8 0.0 slice-done.2
  623.8 0.4 slice-done.3
  624.2 0.0 copy-start.6
  624.2 0.0 copy-start.5
  624.3 0.0 copy-start.4
  624.3 0.0 copy-start.3
  624.3 0.0 copy-start.2
  624.3 0.0 copy-start.1
  624.3 6.3 copy.31
  630.6 0.0 copy-done.6
  630.6 0.9 copy.32
  631.5 0.0 copy-done.5
  631.5 0.9 copy.33
  632.4 0.0 copy-done.4
  632.4 0.9 copy.34
  633.3 0.0 copy-done.3
  633.3 0.9 copy.35
  634.2 0.0 copy-done.2
  634.2 0.9 copy.36
  635.1 0.0 copy-done.1
  635.1 0.9 copy.37
  (1 shorter events, 0.0 us)
Async XLA Ops:
  602.2 15.1 %copy-start = (bf16[2,1024,3328]{2,1,0:T(8,128)(2,1)S(1)}, bf16[2,1024,3328]{2,1,0:T(8,128)(2,1)}, u32[]{:S(2)}) copy-start(bf16[2,1024,3328]{2,1,0:T(8,128)(2,1)} %get-tuple-element.67) | copy-start | bytes 40894468
  602.2 21.6 %slice-start = ((s8[13631488]{0:T(1024)(128)(4,1)}), s8[4194304]{0:T(1024)(128)(4,1)S(1)}, s32[]{:S(2)}) async-start(s8[13631488]{0:T(1024)(128)(4,1)} %bitcast.13), calls=%async_computation | async-start | bytes 8388608
  602.2 21.6 %slice-start.1 = ((s8[13631488]{0:T(1024)(128)(4,1)}), s8[4194304]{0:T(1024)(128)(4,1)S(1)}, s32[]{:S(2)}) async-start(s8[13631488]{0:T(1024)(128)(4,1)} %bitcast.13), calls=%async_computation.1 | async-start | bytes 8388608
  617.3 6.6 %slice-start.2 = ((s8[13631488]{0:T(1024)(128)(4,1)}), s8[4194304]{0:T(1024)(128)(4,1)S(1)}, s32[]{:S(2)}) async-start(s8[13631488]{0:T(1024)(128)(4,1)} %bitcast.13), calls=%async_computation.2 | async-start | bytes 8388608
  617.3 7.0 %slice-start.3 = ((s8[13631488]{0:T(1024)(128)(4,1)}), s8[1048576]{0:T(1024)(128)(4,1)S(1)}, s32[]{:S(2)}) async-start(s8[13631488]{0:T(1024)(128)(4,1)} %bitcast.13), calls=%async_computation.3 | async-start | bytes 2097152
  624.2 6.4 copy-start.6
  624.2 7.3 %copy-start.5 = (f32[2,32,3328]{2,1,0:T(8,128)S(1)}, f32[2,32,3328]{2,1,0:T(8,128)}, u32[]{:S(2)}) copy-start(f32[2,32,3328]{2,1,0:T(8,128)} %get-tuple-element.70) | copy-start | bytes 2555908
  624.3 8.2 %copy-start.4 = (f32[2,104,1024]{2,1,0:T(8,128)S(1)}, f32[2,104,1024]{2,1,0:T(8,128)}, u32[]{:S(2)}) copy-start(f32[2,104,1024]{2,1,0:T(8,128)} %get-tuple-element.71) | copy-start | bytes 2555908
  624.3 9.1 %copy-start.3 = (f32[2,32,3328]{2,1,0:T(8,128)S(1)}, f32[2,32,3328]{2,1,0:T(8,128)}, u32[]{:S(2)}) copy-start(f32[2,32,3328]{2,1,0:T(8,128)} %get-tuple-element.72) | copy-start | bytes 2555908
  624.3 10.0 %copy-start.2 = (f32[2,32,3328]{2,1,0:T(8,128)S(1)}, f32[2,32,3328]{2,1,0:T(8,128)}, u32[]{:S(2)}) copy-start(f32[2,32,3328]{2,1,0:T(8,128)} %get-tuple-element.73) | copy-start | bytes 2555908
  624.3 10.8 %copy-start.1 = (f32[2,104,1024]{2,1,0:T(8,128)S(1)}, f32[2,104,1024]{2,1,0:T(8,128)}, u32[]{:S(2)}) copy-start(f32[2,104,1024]{2,1,0:T(8,128)} %get-tuple-element.74) | copy-start | bytes 2555908

commit v2 on v1

--- a/solution.py
+++ b/solution.py
@@ -90,34 +90,34 @@
     def _(): run(False)
 
 
-XY, YX, ZX, ZY = ("x", "y", "zl", "zh"), ("y", "x", "zl", "zh"), ("zl", "x", "y", "zh"), ("zl", "y", "x", "zh")
-WEIGHT = {"x": 8, "y": 4, "zh": 2, "zl": 1}
-EVENTS = (1, 9, 17, 25, 33, 41, 2, 49, 10, 57, 18, 65, 26, 42, 34, 3, 66, 50, 4, 11, 5, 58, 19, 12, 27, 13, 35, 43, 28, 67, 36, 29, 51, 37, 59, 20, 44, 68, 52, 60, 21, 45, 69, 53, 61)
-DUE = (2, 3, 4, 5, 6, 7, 8, 8, 9, 9, 9, 10, 12, 13, 13, 16, 17, 17, 18, 20, 20, 21, 22, 22, 23, 24, 24, 25, 25, 26, 26, 27, 28, 28, 28, 29, 29, 29, 30, 31, 32, 32, 33, 34, 34)
-
-
-def streams(mats):
-    out = []
-    for m, ref in enumerate(mats):
-        tiles = ref.shape[-1] // 128
-        a, b = 128 * -(-tiles // 3), 128 * (-(-tiles // 3) + -(-(tiles - -(-tiles // 3)) // 2))
-        out += [(m, 0, a, XY), (m, a, b - a, YX), (m, b, 128 * tiles - b, ZY if m % 2 else ZX)]
-    return out
+STREAMS = (
+    (0, 0, 640, ('zl', 'zh', 'x', 'y')),
+    (1, 0, 768, ('x', 'zl', 'y', 'zh')),
+    (1, 768, 1024, ('y', 'x', 'zl', 'zh')),
+    (2, 0, 384, ('zl', 'x', 'y', 'zh')),
+    (2, 384, 384, ('x', 'zl', 'y', 'zh')),
+    (0, 640, 1664, ('y', 'zl', 'zh', 'x')),
+    (0, 2304, 1024, ('y', 'zl', 'x', 'zh')),
+    (1, 1792, 1536, ('x', 'y', 'zl', 'zh')),
+    (2, 768, 256, ('x', 'y', 'zl', 'zh')),
+)
+EVENTS = (1, 9, 17, 25, 33, 2, 10, 41, 49, 18, 57, 65, 26, 34, 3, 11, 19, 42, 35, 20, 50, 58, 12, 43, 21, 36, 51, 66, 13, 59, 44, 27, 37, 67, 4, 60, 52, 68, 28, 45, 5, 61, 53, 69, 29)
+DUE = (0, 1, 1, 2, 2, 2, 3, 3, 3, 4, 4, 5, 5, 5, 6, 6, 6, 7, 7, 8, 9, 9, 10, 10, 10, 10, 11, 11, 11, 12, 12, 12, 12, 13, 13, 13, 13, 13, 13, 14, 14, 14, 14, 14, 15)
 
 
 def sum_scratch(mats):
     out = []
-    for m, _, w, _ in streams(mats):
+    for m, _, w, _ in STREAMS:
         rows = mats[m].shape[-2]
         out += [pltpu.VMEM((2, 8, rows, w), BF), pltpu.VMEM((2, 8, rows, w), BF), pltpu.VMEM((15, rows, w), BF)]
-    n = len(streams(mats))
+    n = len(STREAMS)
     return [*out, pltpu.SemaphoreType.DMA((n,)), pltpu.SemaphoreType.DMA((n, 5)), pltpu.SemaphoreType.DMA((n, 5))]
 
 
 class Sum:
     def __init__(self, here, mats, outs, scratch):
         self.here, self.mats, self.outs = here, mats, outs
-        self.streams = streams(mats)
+        self.streams = STREAMS
         n = len(self.streams)
         self.held = [scratch[3 * s : 3 * s + 3] for s in range(n)]
         self.local, self.sent, self.got = scratch[3 * n :]
@@ -323,10 +323,10 @@
         hid[at_i, :] = (silu * u).astype(BF)
         by_up[at_i, :] = (by_hidden * silu).astype(BF)
         by_gate[at_i, :] = (by_hidden * u * (sigmoid + silu * (1 - sigmoid))).astype(BF)
-    between()
     by_w[0][...] = dot(a_t[...], by_gate[...], (1, 0)).astype(BF)
     by_w[1][...] = dot(a_t[...], by_up[...], (1, 0)).astype(BF)
     by_w[2][...] = dot(by_t[...], hid[...], (1, 0)).T.astype(BF)
+    between()
 
 
 def backward(n, by, by_t, a_t, gate, up, w_down):
@@ -369,17 +369,16 @@
             entry(here)
             total.start()
 
-        def slot(part):
+        def slot():
             for t in range(steps):
-                due = [e for e, at_e in zip(EVENTS, DUE, strict=True) if min(at_e, 2 * steps - 1) == 2 * t + part]
+                due = [e for e, at_e in zip(EVENTS, DUE, strict=True) if min(at_e, steps - 1) == t]
                 if due:
                     @pl.when(step == t)
                     def _(due=due):
                         for code in due:
                             total.event(code)
 
-        of_tile(by, by_t, a_t, gate, up, w_down, hid, by_gate, by_up, by_w, lambda: slot(0))
-        slot(1)
+        of_tile(by, by_t, a_t, gate, up, w_down, hid, by_gate, by_up, by_w, slot)
 
         @pl.when(step == steps - 1)
         def _():
@@ -435,35 +434,26 @@
     return each
 
 
-def stepped(g1, g0, w, m, v):
+def clipping(g1, g0, count):
     g0 = [blocks(t) for t in g0]
-    count = sum(t.size for t in w)
 
     def kernel(*refs):
-        g1, g0, w, m, v = (refs[i : i + 3] for i in range(0, 15, 3))
-        new, new_m, new_v = (refs[i : i + 3] for i in range(15, 24, 3))
-        r0, own_w, stage = (refs[i : i + 3] for i in range(24, 33, 3))
-        norms, load, sends, link, core, nsent, ngot = refs[33:40]
+        g1, g0, r0, factor = refs[:3], refs[3:6], refs[6:9], refs[9]
+        norms, nsent, ngot = refs[10:13]
         here = Place()
-        total = Sum(here, g0, r0, refs[40:])
+        total = Sum(here, g0, r0, refs[13:])
         entry(here)
         total.start()
-
-        def rows_of(ref, p):
-            rows = r0[p // 2].shape[0]
-            return ref.at[p % 2, pl.ds(pl.multiple_of(here.me * rows, 8), rows), :]
-
-        for p in range(6):
-            pltpu.make_async_copy(rows_of(w[p // 2], p), own_w[p // 2].at[p % 2], load.at[p]).start()
         for code in EVENTS:
             total.event(code)
-
         squares = jnp.zeros((8, 128), F32)
         for ref in (*g1, *r0):
+
             def add(cols, so_far, ref=ref):
                 g = ref[:, cols].astype(F32)
                 g = (g * g).reshape(-1, 8, 2, 128)
                 return so_far + jnp.sum(g[:, :, 0] + g[:, :, 1], 0)
+
             squares = tiles(ref)(add)(squares)
         squares = jnp.broadcast_to(jnp.sum(jnp.sum(squares, 0, keepdims=True), 1, keepdims=True), (8, 128))
         for k, to in enumerate(("core", "x", "y", "zl", "zh")):
@@ -472,48 +462,96 @@
             cp.start()
             cp.wait()
             squares = squares + norms[5 + k]
-        factor = jnp.minimum(1.0, 0.5 * lax.rsqrt(squares / count + 1e-30))[:1, :1]
-
+        factor[...] = jnp.minimum(1.0, 0.5 * lax.rsqrt(squares / count + 1e-30))
+        total.finish()
+
+    return pl.pallas_call(
+        kernel,
+        out_shape=[*(jax.ShapeDtypeStruct(t.shape[2:], BF) for t in g0), jax.ShapeDtypeStruct((8, 128), F32)],
+        in_specs=[*[VMEM] * 3, *[ANY] * 3],
+        out_specs=[VMEM] * 4,
+        scratch_shapes=[pltpu.VMEM((10, 8, 128), F32), pltpu.SemaphoreType.DMA((5,)), pltpu.SemaphoreType.DMA((5,)), *sum_scratch(g0)],
+        name="clipping",
+        compiler_params=pltpu.CompilerParams(collective_id=2, has_side_effects=True, vmem_limit_bytes=48 << 20),
+    )(*g1, *g0)
+
+
+def stepped(g1, g0, factor, w, m, v):
+    def kernel(*refs):
+        g1, g0, factor, w, m, v = refs[:3], refs[3:6], refs[6][:1, :1], refs[7:10], refs[10:13], refs[13:16]
+        new, new_m, new_v, own_w, load = refs[16:19], refs[19:22], refs[22:25], refs[25:28], refs[28]
+        me = lax.axis_index("dp")
+
+        def own(p):
+            rows = g0[p // 2].shape[0]
+            src = w[p // 2].at[p % 2, pl.ds(pl.multiple_of(me * rows, 8), rows), :]
+            return pltpu.make_async_copy(src, own_w[p // 2].at[p % 2], load.at[p])
+
+        for p in range(6):
+            own(p).start()
         for p in range(6):
             a, n = p // 2, p % 2
-            pltpu.make_async_copy(rows_of(w[a], p), own_w[a].at[n], load.at[p]).wait()
-            g_ref = (g1 if n else r0)[a]
+            own(p).wait()
+            g_ref = (g1 if n else g0)[a]
 
             def one(cols, _, a=a, n=n, g_ref=g_ref):
                 g = g_ref[:, cols].astype(F32) * factor
                 wide = own_w[a][n, :, cols].astype(F32)
-                stage[a][n, :, cols], new_m[a][n, :, cols], new_v[a][n, :, cols] = adamw(wide, m[a][n, :, cols], v[a][n, :, cols], g)
+                new[a][n, :, cols], new_m[a][n, :, cols], new_v[a][n, :, cols] = adamw(wide, m[a][n, :, cols], v[a][n, :, cols], g)
                 return 0
 
             tiles(g_ref)(one)(0)
-            pltpu.make_async_copy(stage[a].at[n], rows_of(new[a], p), load.at[p]).start()
+
+    state = [jax.ShapeDtypeStruct(t.shape, F32) for t in m]
+    return pl.pallas_call(
+        kernel,
+        out_shape=[*(jax.ShapeDtypeStruct(t.shape, BF) for t in m), *state, *state],
+        in_specs=[*[VMEM] * 7, *[ANY] * 3, *[VMEM] * 6],
+        out_specs=[VMEM] * 9,
+        scratch_shapes=[*(pltpu.VMEM(t.shape, BF) for t in m), pltpu.SemaphoreType.DMA((6,))],
+        name="stepped",
+        compiler_params=pltpu.CompilerParams(vmem_limit_bytes=24 << 20),
+    )(*g1, *g0, factor, *w, *m, *v)
+
+
+def gathered(*own):
+    def kernel(*refs):
+        own, outs, stage = refs[:3], refs[3:6], refs[6:9]
+        load, sends, link, core = refs[9:]
+        here = Place()
+
+        def into(p):
+            return pltpu.make_async_copy(own[p // 2].at[p % 2], stage[p // 2].at[p % 2], load.at[p])
+
+        def out(p):
+            rows = stage[p // 2].shape[1]
+            return pltpu.make_async_copy(stage[p // 2].at[p % 2], outs[p // 2].at[p % 2, pl.ds(pl.multiple_of(here.me * rows, 8), rows), :], load.at[p])
+
         for p in range(6):
-            pltpu.make_async_copy(stage[p // 2].at[p % 2], rows_of(new[p // 2], p), load.at[p]).wait()
-        gather_refs(here, new, sends, link, core)
-        total.finish()
-
-    state = [jax.ShapeDtypeStruct(t.shape, F32) for t in m]
-    return pl.pallas_call(
-        kernel,
-        out_shape=[*(jax.ShapeDtypeStruct(t.shape, BF) for t in w), *state, *state],
-        in_specs=[*[VMEM] * 3, *[ANY] * 6, *[VMEM] * 6],
-        out_specs=[*[ANY] * 3, *[VMEM] * 6],
+            into(p).start()
+        entry(here)
+        for p in range(6):
+            into(p).wait()
+            out(p).start()
+        for p in range(6):
+            out(p).wait()
+        gather_refs(here, outs, sends, link, core)
+
+    return pl.pallas_call(
+        kernel,
+        out_shape=[jax.ShapeDtypeStruct((2, 32 * t.shape[1], t.shape[2]), BF) for t in own],
+        in_specs=[ANY] * 3,
+        out_specs=[ANY] * 3,
         scratch_shapes=[
-            *(pltpu.VMEM(t.shape[2:], BF) for t in g0),
-            *(pltpu.VMEM(t.shape, BF) for t in m),
-            *(pltpu.VMEM(t.shape, BF) for t in m),
-            pltpu.VMEM((10, 8, 128), F32),
+            *(pltpu.VMEM(t.shape, BF) for t in own),
             pltpu.SemaphoreType.DMA((6,)),
             pltpu.SemaphoreType.DMA((240,)),
             pltpu.SemaphoreType.DMA((6, 16)),
             pltpu.SemaphoreType.DMA((6, 16)),
-            pltpu.SemaphoreType.DMA((5,)),
-            pltpu.SemaphoreType.DMA((5,)),
-            *sum_scratch(g0),
         ],
-        name="stepped",
-        compiler_params=pltpu.CompilerParams(collective_id=2, has_side_effects=True, vmem_limit_bytes=63 << 20),
-    )(*g1, *g0, *w, *m, *v)
+        name="gathered",
+        compiler_params=pltpu.CompilerParams(collective_id=3, has_side_effects=True, vmem_limit_bytes=8 << 20),
+    )(*own)
 
 
 def dot(a, b, contract):
@@ -543,7 +581,9 @@
         *g1, by_gate, by_up = backward(1, by, by_t, a1_t, gate1, up1, w[2])
         by, by_t = backward_states(1, by_gate, by_up, w[0], w[1], h1, by)
         both = backward_beside(g1, 0, by, by_t, a0_t, gate0, up0, w[2])
-        return tuple(stepped(both[3:], both[:3], w, m, v))
+        *g0, factor = clipping(both[3:], both[:3], sum(t.size for t in w))
+        new = stepped(both[3:], g0, factor, w, m, v)
+        return (*gathered(*new[:3]), *new[3:])
 
     rows = P(None, "dp", None)
     return jax.shard_map(

time: 636 us -> 618 us (0.972)
  local copies, waits for them, and re-layouts: 33.8 us -> 23.7 us
  Pallas kernels: 602 us -> 593 us
    pallas_call x0 -> x2, Pallas kernels: none -> 259 us  [the longest x1 155 us: gathered(): pl.pallas_call(kernel, out_shape=[jax.ShapeDtypeStruct((2, 32 * t.shape[1...]
    pallas_call x1, Pallas kernels: 264 us -> 5.29 us  [stepped(): pl.pallas_call(kernel, out_shape=[*(jax.ShapeDtypeStruct(t.shape, BF) for...]
    unnamed x31 -> x23, local copies, waits for them, and re-layouts: 33.8 us -> 23.7 us
    pallas_call x1, Pallas kernels: 115 us -> 106 us  [backward_beside(): pl.pallas_call(kernel, grid=(steps,), out_shape=[*(jax.ShapeDtypeStruct(s...]
where the time goes in v2:
time: 618 us
  Pallas kernels  593 us (96%)
  local copies, waits for them, and re-layouts  23.7 us (4%)
    pallas_call x1, Pallas kernels, gathered(): pl.pallas_call(kernel, out_shape=[jax.ShapeDtypeStruct((2, 32 * t.shape[1...  155 us
    pallas_call x1, Pallas kernels, backward_beside(): pl.pallas_call(kernel, grid=(steps,), out_shape=[*(jax.ShapeDtypeStruct(s...  106 us
    pallas_call x1, Pallas kernels, clipping(): pl.pallas_call(kernel, out_shape=[*(jax.ShapeDtypeStruct(t.shape[2:], BF)...  104 us
    pallas_call x1, Pallas kernels, backward(): pl.pallas_call(kernel, grid=(ff // TILE,), out_shape=[jax.ShapeDtypeStruc...  77.2 us
    pallas_call x2, Pallas kernels, forward_up(): pl.pallas_call(kernel, grid=(ff // TILE,), out_shape=[jax.ShapeDtypeStruc...  71.1 us
    pallas_call x1, Pallas kernels, backward_states(): pl.pallas_call(kernel, grid=(tokens // rows,), out_shape=[jax.ShapeDtypeS...  41.6 us
    unnamed x23, local copies, waits for them, and re-layouts  23.7 us
    pallas_call x1, Pallas kernels, forward_down(): pl.pallas_call(kernel, grid=(tokens // rows,), out_shape=[flat, flat, tur...  23.3 us

profile of v2, /device:TPU:1, one launch (start us, length us, event | category | flops | bytes accessed | tf_op | source)
XLA Modules:
  0.0 617.6 jit_solution(14269896372531426487)
XLA Ops:
  0.6 9.0 %prepared.1 = (bf16[2048,1024]{1,0:T(8,128)(2,1)}, bf16[1024,2048]{1,0:T(8,128)(2,1)}, bf16[1024,2048]{1,0:T(8,128)(2,1)}) custom-call(bf16[2048,1024]{1,0:T(8,128)(2,1)} %bitcast.11, bf16[2048,1024]{1,0:T(8,128)(2,1)} %bitcast.8), custom_call_target="tpu_custom_call" | custom-call | tf_op jit(solution)/shard_map/prepared/pallas_call | solution.py:256
  9.6 35.8 %forward_up.2 = (f32[2048,3328]{1,0:T(8,128)}, f32[2048,3328]{1,0:T(8,128)}, bf16[2048,3328]{1,0:T(8,128)(2,1)}) custom-call(bf16[2048,1024]{1,0:T(8,128)(2,1)} %get-tuple-element.50.a, bf16[2,1024,3328]{2,1,0:T(8,128)(2,1)} %refs_7_.1, bf16[2,1024,3328]{2,1,0:T(8,128)(2,1)} %refs_8_.1), custom_call_target="tpu_custom_call" | custom-call | tf_op jit(solution)/shard_map/forward_up/pallas_call | solution.py:281
  45.4 23.3 %forward_down.1 = (bf16[2048,1024]{1,0:T(8,128)(2,1)}, bf16[2048,1024]{1,0:T(8,128)(2,1)}, bf16[1024,2048]{1,0:T(8,128)(2,1)}) custom-call(bf16[2048,3328]{1,0:T(8,128)(2,1)} %get-tuple-element.51.hidden, bf16[2,3328,1024]{2,1,0:T(8,128)(2,1)} %refs_9_.1, bf16[2048,1024]{1,0:T(8,128)(2,1)} %bitcast.12), custom_call_target="tpu_custom_call" | custom-call | tf_op jit(solution)/shard_map/forward_down/pallas_call | solution.py:304
  68.7 35.3 %forward_up.3 = (f32[2048,3328]{1,0:T(8,128)}, f32[2048,3328]{1,0:T(8,128)}) custom-call(bf16[2048,1024]{1,0:T(8,128)(2,1)} %get-tuple-element.53.a, bf16[2,1024,3328]{2,1,0:T(8,128)(2,1)} %refs_7_.1, bf16[2,1024,3328]{2,1,0:T(8,128)(2,1)} %refs_8_.1), custom_call_target="tpu_custom_call" | custom-call | tf_op jit(solution)/shard_map/forward_up/pallas_call | solution.py:281
  104.0 77.2 %backward.1 = (bf16[1024,3328]{1,0:T(8,128)(2,1)}, bf16[1024,3328]{1,0:T(8,128)(2,1)}, bf16[3328,1024]{1,0:T(8,128)(2,1)}, bf16[2048,3328]{1,0:T(8,128)(2,1)}, bf16[2048,3328]{1,0:T(8,128)(2,1)}) custom-call(bf16[2048,1024]{1,0:T(8,128)(2,1)} %bitcast.9, bf16[1024,2048]{1,0:T(8,128)(2,1)} %get-tuple-element.49.by_t, ...), custom_call_target="tpu_custom_call" | custom-call | tf_op jit(solution)/shard_map/backward/pallas_call | solution.py:341
  181.2 41.6 %backward_states.1 = (bf16[2048,1024]{1,0:T(8,128)(2,1)}, bf16[1024,2048]{1,0:T(8,128)(2,1)}) custom-call(bf16[2048,3328]{1,0:T(8,128)(2,1)} %get-tuple-element.56.by_gate, bf16[2048,3328]{1,0:T(8,128)(2,1)} %get-tuple-element.57.by_up, bf16[2,1024,3328]{2,1,0:T(8,128)(2,1)} %refs_7_.1, bf16[2,1024,3328]{2,1,0:T(8,128)(2,1)} %refs_8_.1, ...), custom_call_target="tpu_custom_call" | custom-call | tf_op jit(solution)/shard_map/backward_states/pallas_call | solution.py:416
  222.7 106.3 %backward_beside.1 = (bf16[1024,3328]{1,0:T(8,128)(2,1)}, bf16[1024,3328]{1,0:T(8,128)(2,1)}, bf16[3328,1024]{1,0:T(8,128)(2,1)}, bf16[32,3328]{1,0:T(8,128)(2,1...) custom-call(bf16[2048,1024]{1,0:T(8,128)(2,1)} %get-tuple-element.59.refs_0_, ...), custom_call_target="tpu_custom_call" | custom-call | tf_op jit(solution)/shard_map/backward_beside/pallas_call | solution.py:388
  329.0 0.0 copy-start.1
  329.0 0.0 copy-start.2
  329.0 0.0 copy-start.3
  329.1 0.0 copy-start.4
  329.1 0.0 copy-start.5
  329.1 0.0 copy-start.6
  329.1 0.0 copy-start.7
  329.1 1.1 copy-done.7
  330.2 0.0 copy-start.8
  330.2 1.4 copy-done.8
  331.6 0.0 copy-start.9
  331.6 0.9 copy-done.9
  332.5 104.0 %clipping.1 = (bf16[32,3328]{1,0:T(8,128)(2,1)S(1)}, bf16[32,3328]{1,0:T(8,128)(2,1)S(1)}, bf16[104,1024]{1,0:T(8,128)(2,1)S(1)}, f32[8,128]{1,0:T(8,128)S(1)}) custom-call(bf16[32,3328]{1,0:T(8,128)(2,1)S(1)} %copy-done.7, bf16[32,3328]{1,0:T(8,128)(2,1)S(1)} %copy-done.8, bf16[104,1024]{1,0:T(8,128)(2,1)S(1)} %copy-done.9, ...), custom_call_target="tpu_custom_call" | custom-call | tf_op jit(solution)/shard_map/clipping/pallas_call | solution.py:468
  436.5 0.0 copy-done.1
  436.5 0.0 copy-done.2
  436.5 0.0 copy-done.3
  436.6 0.0 copy-done.4
  436.6 0.0 copy-done.5
  436.6 0.0 copy-done.6
  436.6 0.0 copy-start
  436.6 4.9 copy-done
  441.5 5.3 stepped.1
  446.8 155.4 %gathered.1 = (bf16[2,1024,3328]{2,1,0:T(8,128)(2,1)S(1)}, bf16[2,1024,3328]{2,1,0:T(8,128)(2,1)S(1)}, bf16[2,3328,1024]{2,1,0:T(8,128)(2,1)S(1)}) custom-call(bf16[2,32,3328]{2,1,0:T(8,128)(2,1)S(1)} %get-tuple-element.77.refs_0_, bf16[2,32,3328]{2,1,0:T(8,128)(2,1)S(1)} %get-tuple-element.78.refs_1_, bf16[2,104,1024]{2,1,0:T(8,128)(2,1)S(1)} %get-tuple-element.79.refs_2_), custom_call_target="tpu_custom_call" | custom-call | tf_op jit(solution)/shard_map/gathered/pallas_call | solution.py:540
  602.2 5.1 copy.23
  607.3 5.1 copy.24
  612.4 5.1 copy.25
Async XLA Ops:
  329.0 107.5 %copy-start.1 = (f32[2,32,3328]{2,1,0:T(8,128)S(1)}, f32[2,32,3328]{2,1,0:T(8,128)}, u32[]{:S(2)}) copy-start(f32[2,32,3328]{2,1,0:T(8,128)} %refs_10_.1) | copy-start | bytes 2555908
  329.0 107.5 %copy-start.2 = (f32[2,32,3328]{2,1,0:T(8,128)S(1)}, f32[2,32,3328]{2,1,0:T(8,128)}, u32[]{:S(2)}) copy-start(f32[2,32,3328]{2,1,0:T(8,128)} %refs_11_.1) | copy-start | bytes 2555908
  329.0 107.5 %copy-start.3 = (f32[2,104,1024]{2,1,0:T(8,128)S(1)}, f32[2,104,1024]{2,1,0:T(8,128)}, u32[]{:S(2)}) copy-start(f32[2,104,1024]{2,1,0:T(8,128)} %refs_12_.1) | copy-start | bytes 2555908
  329.1 107.5 %copy-start.4 = (f32[2,32,3328]{2,1,0:T(8,128)S(1)}, f32[2,32,3328]{2,1,0:T(8,128)}, u32[]{:S(2)}) copy-start(f32[2,32,3328]{2,1,0:T(8,128)} %refs_13_.1) | copy-start | bytes 2555908
  329.1 107.5 %copy-start.5 = (f32[2,32,3328]{2,1,0:T(8,128)S(1)}, f32[2,32,3328]{2,1,0:T(8,128)}, u32[]{:S(2)}) copy-start(f32[2,32,3328]{2,1,0:T(8,128)} %refs_14_.1) | copy-start | bytes 2555908
  329.1 107.5 %copy-start.6 = (f32[2,104,1024]{2,1,0:T(8,128)S(1)}, f32[2,104,1024]{2,1,0:T(8,128)}, u32[]{:S(2)}) copy-start(f32[2,104,1024]{2,1,0:T(8,128)} %refs_15_.1) | copy-start | bytes 2555908
  329.1 1.1 copy-start.7
  330.2 1.4 copy-start.8
  331.6 0.9 copy-start.9
  436.6 4.9 copy-start
